TPU v7x, 512 devices: a whole 4x8x8 slice. The times are simulated.
512 devices in a mesh: row: 16 (over z, core), col: 32 (over y, x).
Axes of the slice: x: 4, y: 8, z: 8, core: 2. Of those that a mesh axis runs over, the one named last changes fastest.
Arguments:
- matrix: float32 [15360, 15360], P('row', 'col'), may hold values from -4 to 4
- rhs: float32 [15360, 4096], P('row', 'col'), may hold values from -6 to 6
- pivot_inverses: bfloat16 [2, 512, 512], replicated, may hold values from -0.046875 to 0.046875
- panel_order: int32 [2], replicated, may hold values from 0 to 29, as said below
Outputs:
- factored: bfloat16 [15360, 15360], P('row', 'col')
- updated_rhs: float32 [15360, 4096], P('row', 'col')
- rhs_norms: float32 [4096], P('col')
Inputs may be any that keep to these rules, and one draw needn't show every extreme that they name: `panel_order`: two different panel indices, one of which is the last panel, 29.
All inputs are finite; a program needn't handle non-finite values.
Results may differ from a plain program's by a relative error of at most 0.001.
Values sent between devices are 32-bit elements; how exact they have to be, the bound alone decides.
A program may use at most 64 MiB of HBM per device.

v0:
```python
import functools

import jax
import jax.numpy as jnp
from jax import lax
from jax.experimental import pallas as pl
from jax.experimental.pallas import tpu as pltpu
from jax.sharding import Mesh
from jax.sharding import PartitionSpec as P

N = 15360
PW = 512
NB = 32
NZ, NC, NY, NX = 8, 2, 8, 4
PARTS = 16
MIB = 2**20
PIECES = 2
ROWS = 1024
MESH = pl.DeviceIdType.MESH


def gather_kernel(
    halves, ct_ref, u_ref, strip_ref, ct_all, u_all, t_all, strips,
    s_b, r_b, s_a, r_a, s_u, r_u, s_t, r_t, s_y, r_y, s_x, r_x
):
    z, c = lax.axis_index("z"), lax.axis_index("core")
    y, x = lax.axis_index("y"), lax.axis_index("x")
    panels = len(halves)
    cut, pieces = (256, PIECES) if halves[0] != halves[1] else (128, 1)
    step_lanes = -(-(ROWS - cut) // (128 * pieces)) * 128
    cuts = [*range(cut, ROWS, step_lanes), ROWS]
    spans = [pl.ds(lo, hi - lo) for lo, hi in zip(cuts[:-1], cuts[1:])]

    def along(axis, step):
        size = {"z": NZ, "core": NC, "y": NY, "x": NX}[axis]
        here = {"z": z, "core": c, "y": y, "x": x}[axis]
        return {axis: lax.rem(here + step + size, size)}

    barrier = pltpu.get_barrier_semaphore()
    peers = [("y", step) for step in range(1, NY)] + [("x", step) for step in range(1, NX)]
    peers += [("z", 1), ("z", -1), ("core", 1)]
    for axis, step in peers:
        pl.semaphore_signal(barrier, inc=1, device_id=along(axis, step), device_id_type=MESH)
    pl.semaphore_wait(barrier, len(peers))

    def copy(src, dst, s_sem, r_sem, target):
        return pltpu.make_async_remote_copy(
            src_ref=src, dst_ref=dst, send_sem=s_sem, recv_sem=r_sem, device_id=target, device_id_type=MESH
        )

    def low(p, k):
        return ct_all.at[p, k, :, pl.ds(0, cut)]

    def high(p, k, n):
        return ct_all.at[p, k, :, spans[n]]

    def send_low(p, k, d, target, src=None):
        return copy(low(p, k) if src is None else src, low(p, k), s_a.at[p, k, d], r_a.at[p, k], target)

    def send_high(p, k, n, d, target, own=False):
        slot = high(p, k, n)
        src = ct_ref.at[p, :, spans[n]] if own else slot
        return copy(src, slot, s_b.at[p, k, n, d], r_b.at[p, k, n], target)

    def send_u(part, d, target, src=None):
        slot = u_all.at[:, part]
        return copy(slot if src is None else src, slot, s_u.at[part, d], r_u.at[part], target)

    def send_t(part, d, target):
        slot = t_all.at[:, part]
        return copy(slot, slot, s_t.at[part, d], r_t.at[part], target)

    def send_strip(p, j, step):
        slot = strips.at[p, x, j]
        return copy(strip_ref.at[p], slot, s_y.at[p, step], r_y.at[p, j], along("y", step))

    def send_strips(p, where, step):
        slot = strips.at[p, where]
        return copy(slot, slot, s_x.at[p, step], r_x.at[p, where], along("x", step))

    def reach(j, way):
        long_way = (j >= 2) if way > 0 else (j < 2)
        return jnp.where(long_way, *((4, 3) if halves[0] != halves[1] else (5, 2)))

    def distance(p):
        return lax.rem(y - 4 * halves[p] + 8, 8)

    def source_at(p, t, way):
        return lax.rem(y - way * t - 4 * halves[p] + 16, 8)

    def other_x(step):
        return lax.rem(x + step + NX, NX)

    def cross(p, j, drain):
        first, second = 4 * j + other_x(-1), 4 * j + other_x(1)
        even = lax.rem(j, 2) == 0
        for n in range(len(spans)):
            if not drain:
                send_high(p, first, n, 0, along("x", 1)).wait_recv()
                send_high(p, second, n, 0, along("x", 1)).wait_recv()

            @pl.when(even)
            def _(n=n):
                op = send_high(p, first, n, 2, along("x", 1))
                op.wait_send() if drain else op.start()

            @pl.when(jnp.logical_not(even))
            def _(n=n):
                op = send_high(p, second, n, 3, along("x", -1))
                op.wait_send() if drain else op.start()

    def spread(p, k, n, drain, own=False):
        for d, step in ((2, 1), (3, -1)):
            op = send_high(p, k, n, d, along("x", step), own)
            op.wait_send() if drain else op.start()

    def strips_along_y(drain):
        for p in range(panels):
            j = distance(p)

            @pl.when(j < 4)
            def _(p=p, j=j):
                for step in range(1, NY):
                    op = send_strip(p, j, step)
                    op.wait_send() if drain else op.start()
                if not drain:
                    strips[p, x, j] = strip_ref[p]

    def strips_along_x(drain):
        for p in range(panels):
            if not drain:

                def arrive(j, _, p=p):
                    @pl.when(j != distance(p))
                    def _():
                        send_strip(p, j, 1).wait_recv()

                    return 0

                lax.fori_loop(0, 4, arrive, 0)
            for step in range(1, NX):
                op = send_strips(p, x, step)
                op.wait_send() if drain else op.start()

    def join_strips():
        lane = lax.broadcasted_iota(jnp.int32, (8, 128), 1) // NB
        for p in range(panels):
            for step in range(1, NX):
                send_strips(p, other_x(step), step).wait_recv()
            for j in range(4):
                parts = [strips[p, e, j] for e in range(NX)]
                for q in range(4):
                    joined = parts[q]
                    for e in range(NX):
                        if e != q:
                            joined = jnp.where(lane == e, pltpu.roll(parts[e], NB * ((e - q) % 4), 1), joined)
                    t_all[p, mine, 8 * q : 8 * q + 8, 128 * j : 128 * j + 128] = joined

    mine = 2 * z + c

    def own_t(drain):
        for d, target in ((0, along("z", 1)), (1, along("z", -1)), (2, along("core", 1))):
            op = send_t(mine, d, target)
            op.wait_send() if drain else op.start()

    def z_step(send, t, drain):
        far_z = {1: 4, -1: 3}
        for way, d in ((1, 0), (-1, 1)):

            @pl.when(t <= far_z[way])
            def _(way=way, d=d):
                part = 2 * lax.rem(z - way * t + NZ, NZ) + c
                if not drain:
                    send(part, d, along("z", way)).wait_recv()

                @pl.when(t + 1 <= far_z[way])
                def _():
                    op = send(part, d, along("z", way))
                    op.wait_send() if drain else op.start()

                op = send(part, 2, along("core", 1))
                op.wait_send() if drain else op.start()

    def own_step(drain):
        for d, target in ((0, along("z", 1)), (1, along("z", -1)), (2, along("core", 1))):
            op = send_u(mine, d, target, u_ref)
            op.wait_send() if drain else op.start()
        for p in range(panels):
            j = distance(p)

            @pl.when(j < 4)
            def _(p=p, j=j):
                k = 4 * j + x
                own_low = ct_ref.at[p, :, pl.ds(0, cut)]
                for d, step in ((2, 1), (3, -1), (4, 2)):
                    op = send_low(p, k, d, along("x", step), own_low)
                    op.wait_send() if drain else op.start()
                for n in range(len(spans)):
                    for d, step in ((0, 1), (1, -1)):
                        op = send_high(p, k, n, d, along("y", step), True)
                        op.wait_send() if drain else op.start()
                    spread(p, k, n, drain, True)
                for d, step in ((0, 1), (1, -1)):
                    op = send_low(p, k, d, along("y", step), own_low)
                    op.wait_send() if drain else op.start()
        if not drain:
            u_all[:, mine] = u_ref[...]
            for p in range(panels):

                @pl.when(distance(p) < 4)
                def _(p=p):
                    ct_all[p, 4 * distance(p) + x] = ct_ref[p]

        for p in range(panels):
            j = distance(p)

            @pl.when(j < 4)
            def _(p=p, j=j):
                for e in (1, 3, 2):
                    k = 4 * j + other_x(e)
                    if not drain:
                        send_low(p, k, 0, along("y", 1)).wait_recv()
                    for d, step in ((0, 1), (1, -1)):
                        op = send_low(p, k, d, along("y", step))
                        op.wait_send() if drain else op.start()

    def ring_step(t, drain):
        for way, d in ((1, 0), (-1, 1)):
            for p in range(panels):
                j = source_at(p, t, way)
                far = reach(j, way)

                @pl.when((j < 4) & (t <= far))
                def _(p=p, j=j, far=far, way=way, d=d):
                    k = 4 * j + x
                    for n in range(len(spans)):
                        if not drain:
                            send_high(p, k, n, d, along("y", way)).wait_recv()

                        @pl.when(t + 1 <= far)
                        def _(n=n):
                            op = send_high(p, k, n, d, along("y", way))
                            op.wait_send() if drain else op.start()

                        spread(p, k, n, drain)
        z_step(send_u, t, drain)
        for way, d in ((1, 0), (-1, 1)):
            for p in range(panels):
                j = source_at(p, t, way)
                far = reach(j, way)

                @pl.when((j < 4) & (t <= far))
                def _(p=p, j=j, far=far, way=way, d=d):
                    for e in range(NX):
                        k = 4 * j + other_x(e)
                        if not drain:
                            send_low(p, k, d, along("y", way)).wait_recv()

                        @pl.when(t + 1 <= far)
                        def _(k=k):
                            op = send_low(p, k, d, along("y", way))
                            op.wait_send() if drain else op.start()

    def cross_step(t, drain):
        for way in (1, -1):
            for p in range(panels):
                j = source_at(p, t, way)

                @pl.when((j < 4) & (t <= reach(j, way)))
                def _(p=p, j=j):
                    cross(p, j, drain)

    def cross_own(drain):
        for p in range(panels):

            @pl.when(distance(p) < 4)
            def _(p=p):
                cross(p, distance(p), drain)

    def whole(drain):
        strips_along_y(drain)
        own_step(drain)
        strips_along_x(drain)
        cross_own(drain)

        def body(t, _):
            ring_step(t, drain)

            @pl.when(t == 1)
            def _():
                if not drain:
                    join_strips()
                own_t(drain)

            @pl.when(t > 1)
            def _():
                cross_step(t - 1, drain)
                z_step(send_t, t - 1, drain)

            return 0

        lax.fori_loop(1, 6, body, 0)
        cross_step(5, drain)

    whole(False)

    def last(j, _):
        for p in range(panels):
            for n in range(len(spans)):
                send_high(p, 4 * j + other_x(2), n, 0, along("x", 1)).wait_recv()
        return 0

    lax.fori_loop(0, 4, last, 0)

    def sibling(i, _):
        send_u(2 * i + 1 - c, 2, along("core", 1)).wait_recv()
        send_t(2 * i + 1 - c, 2, along("core", 1)).wait_recv()
        return 0

    lax.fori_loop(0, NZ, sibling, 0)
    whole(True)


def gather_panels(halves, ident, ct, u, strip):
    panels, width = ct.shape[0], u.shape[-1]
    dma = pltpu.SemaphoreType.DMA
    return pl.pallas_call(
        functools.partial(gather_kernel, halves),
        out_shape=(
            jax.ShapeDtypeStruct((panels, PARTS, NB, ROWS), jnp.float32),
            jax.ShapeDtypeStruct((panels, PARTS, NB, width), jnp.float32),
            jax.ShapeDtypeStruct((panels, PARTS, NB, PW), jnp.float32),
        ),
        in_specs=[pl.BlockSpec(memory_space=pltpu.VMEM)] * 3,
        out_specs=[pl.BlockSpec(memory_space=pltpu.VMEM)] * 3,
        scratch_shapes=[
            pltpu.VMEM((panels, NX, 4, 8, 128), jnp.float32),
            dma((panels, PARTS, PIECES, 4)),
            dma((panels, PARTS, PIECES)),
            dma((panels, PARTS, 5)),
            dma((panels, PARTS)),
            dma((PARTS, 3)),
            dma((PARTS,)),
            dma((PARTS, 3)),
            dma((PARTS,)),
            dma((panels, NY)),
            dma((panels, 4)),
            dma((panels, NX)),
            dma((panels, NX)),
        ],
        compiler_params=pltpu.CompilerParams(
            collective_id=ident, has_side_effects=True, vmem_limit_bytes=14 * MIB
        ),
        name=f"gather_{ident}",
    )(ct, u, strip)


def halved(value):
    high = value.astype(jnp.bfloat16)
    return high, (value - high.astype(jnp.float32)).astype(jnp.bfloat16)


def dot(first, second):
    return jnp.dot(first, second, preferred_element_type=jnp.float32)


def dot_2(first, second):
    high, low = halved(second)
    return dot(first, low) + dot(first, high)


def dot_3(first, second):
    high, low = halved(first)
    high_2, low_2 = halved(second)
    return dot(high, low_2) + dot(low, high_2) + dot(high, high_2)


def finish_kernel(
    order_ref, v_ref, t_ref, u_ref, ct_hbm, a, r, a_out, r_out, n_out,
    ct, z_high, z_low, ct_high, ct_low, y_ref, update, part_ref, held, load, send, recv
):
    z, c = lax.axis_index("z"), lax.axis_index("core")
    mine = 2 * z + c
    col_index = NX * lax.axis_index("y") + lax.axis_index("x")
    row_len, col_len = a_out.shape
    width = u_ref.shape[2]

    def peer(step):
        there = lax.rem(mine + step, PARTS)
        return {"z": there // 2, "core": lax.rem(there, 2)}

    barrier = pltpu.get_barrier_semaphore()
    for step in range(1, PARTS):
        pl.semaphore_signal(barrier, inc=1, device_id=peer(step), device_id_type=MESH)
    loading = pltpu.make_async_copy(ct_hbm, ct, load)
    loading.start()

    first, second = order_ref[0], order_ref[1]
    col = lax.broadcasted_iota(jnp.int32, (PW, width), 1)
    row = lax.broadcasted_iota(jnp.int32, (PW, width), 0)
    minus_one = jnp.where(row == lax.rem(col_index, PARTS) * NB + (col & (NB - 1)), -1.0, 0.0)

    def hit(panel_id):
        there = jnp.where(col_index // PARTS == (panel_id & 1), panel_id >> 1, -1)
        return (col >> 5) == there

    hit_1, hit_2 = hit(first), hit(second)
    w_1 = dot_2(v_ref[0], jnp.where(hit_1, minus_one, u_ref[0]))
    y_2 = jnp.where(hit_1, 0.0, u_ref[1]) - dot_3(t_ref[0], w_1)
    y_ref[...] = y_2
    w_2 = dot_2(v_ref[1], jnp.where(hit_2, minus_one, jnp.where(hit_1, 0.0, y_2)))
    z_high[PW:], z_low[PW:] = halved(w_2)
    z_1 = jnp.where(hit_2, 0.0, w_1) - dot_3(dot_2(v_ref[0], t_ref[1]), w_2)
    z_high[:PW], z_low[:PW] = halved(z_1)
    loading.wait()
    ct_high[...], ct_low[...] = halved(ct[...].T)

    def multiply(start, length):
        cols = slice(start, start + length)
        return (
            dot(ct_high[...], z_low[:, cols])
            + dot(ct_low[...], z_high[:, cols])
            + dot(ct_high[...], z_high[:, cols])
        )

    update[:, PW:] = multiply(PW, width - PW)
    kept = y_ref[pl.ds(pl.multiple_of(mine * NB, NB), NB), :]

    def right_block(b, total):
        here = pl.ds(pl.multiple_of(b * NB, NB), NB)
        old = r[here, :]
        new = jnp.where(b == first, old, jnp.where(b == second, kept[:, PW:], old - update[here, PW:]))
        r_out[here, :] = new
        return total + new * new

    total = lax.fori_loop(0, row_len // NB, right_block, jnp.zeros((NB, width - PW), jnp.float32))
    part_ref[...] = jnp.broadcast_to(jnp.sum(total, axis=0, keepdims=True), part_ref.shape)
    pl.semaphore_wait(barrier, PARTS - 1)

    def copy(step):
        return pltpu.make_async_remote_copy(
            src_ref=part_ref, dst_ref=held.at[step], send_sem=send.at[step], recv_sem=recv.at[step],
            device_id=peer(step), device_id_type=MESH,
        )

    for step in range(1, PARTS):
        copy(step).start()
    update[:, :PW] = multiply(0, PW)
    cleared = jnp.where(hit_1 | hit_2, 0.0, 1.0)[:NB, :col_len]

    def left_block(b, _):
        here = pl.ds(pl.multiple_of(b * NB, NB), NB)
        old = a[here, :]
        new = jnp.where(
            b == first, old, jnp.where(b == second, kept[:, :col_len], old * cleared - update[here, :col_len])
        )
        a_out[here, :] = new.astype(jnp.bfloat16)
        return 0

    lax.fori_loop(0, row_len // NB, left_block, 0)
    squares = part_ref[...]
    for step in range(1, PARTS):
        copy(step).wait_recv()
        squares = squares + held[step]
    n_out[...] = jnp.sqrt(squares / N + 1e-06)
    for step in range(1, PARTS):
        copy(step).wait_send()


def finish(order, inverses, t, u, ct, matrix, rhs):
    dma = pltpu.SemaphoreType.DMA
    (row_len, col_len), extra, width = matrix.shape, rhs.shape[1], u.shape[2]
    vmem = pl.BlockSpec(memory_space=pltpu.VMEM)
    depth = ct.shape[0]
    return pl.pallas_call(
        finish_kernel,
        out_shape=(
            jax.ShapeDtypeStruct(matrix.shape, jnp.bfloat16),
            jax.ShapeDtypeStruct(rhs.shape, jnp.float32),
            jax.ShapeDtypeStruct((8, extra), jnp.float32),
        ),
        in_specs=[pl.BlockSpec(memory_space=pltpu.SMEM), *[vmem] * 3, pl.BlockSpec(memory_space=pl.ANY), vmem, vmem],
        out_specs=[vmem] * 3,
        scratch_shapes=[
            pltpu.VMEM(ct.shape, jnp.float32),
            pltpu.VMEM((depth, width), jnp.bfloat16),
            pltpu.VMEM((depth, width), jnp.bfloat16),
            pltpu.VMEM(ct.shape[::-1], jnp.bfloat16),
            pltpu.VMEM(ct.shape[::-1], jnp.bfloat16),
            pltpu.VMEM((PW, width), jnp.float32),
            pltpu.VMEM((ct.shape[1], width), jnp.float32),
            pltpu.VMEM((8, extra), jnp.float32),
            pltpu.VMEM((PARTS, 8, extra), jnp.float32),
            dma,
            dma((PARTS,)),
            dma((PARTS,)),
        ],
        compiler_params=pltpu.CompilerParams(
            collective_id=9, has_side_effects=True, vmem_limit_bytes=40 * MIB
        ),
        name="finish",
    )(order, inverses, t, u, ct, matrix, rhs)


def prepare_kernel(order_ref, a_ref, r_ref, ct_out, u_out, strip_out, wide):
    row_len, col_len = a_ref.shape
    wide[:row_len, :col_len] = a_ref[...]
    wide[row_len:, :] = jnp.zeros((ROWS - row_len, PW), jnp.float32)
    lane = lax.broadcasted_iota(jnp.int32, (8, 128), 1) // NB
    for p in range(2):
        own, other = order_ref[p], order_ref[1 - p]
        block = own >> 1
        tile = pl.ds(pl.multiple_of((block >> 2) * 128, 128), 128)
        shift = (128 - (block & 3) * NB) & 127
        here, there = (pl.ds(pl.multiple_of(n * NB, NB), NB) for n in (own, other))
        ct_out[p] = pltpu.roll(wide[:, tile], shift, 1).T[:NB]
        u_out[p, :, :PW] = wide[here, :]
        u_out[p, :, PW:] = r_ref[here, :]
        cross = pltpu.roll(wide[there, tile], shift, 1)
        joined = cross[:8]
        for q in range(1, 4):
            joined = jnp.where(lane == q, pltpu.roll(cross[8 * q : 8 * q + 8], NB * q, 1), joined)
        strip_out[p] = joined


def prepare(order, matrix, rhs):
    vmem = pl.BlockSpec(memory_space=pltpu.VMEM)
    return pl.pallas_call(
        prepare_kernel,
        out_shape=(
            jax.ShapeDtypeStruct((2, NB, ROWS), jnp.float32),
            jax.ShapeDtypeStruct((2, NB, PW + rhs.shape[1]), jnp.float32),
            jax.ShapeDtypeStruct((2, 8, 128), jnp.float32),
        ),
        in_specs=[pl.BlockSpec(memory_space=pltpu.SMEM), vmem, vmem],
        out_specs=[vmem] * 3,
        scratch_shapes=[pltpu.VMEM((ROWS, PW), jnp.float32)],
        compiler_params=pltpu.CompilerParams(vmem_limit_bytes=14 * MIB),
        name="prepare",
    )(order, matrix, rhs)


def on_device(matrix, rhs, pivot_inverses, panel_order):
    width = PW + rhs.shape[1]
    ct, u, strip = prepare(panel_order, matrix, rhs)
    branch = jnp.sum((panel_order & 1) * jnp.array([2, 1], jnp.int32)) - 1
    ct_all, u_all, t_all = lax.switch(
        branch, [functools.partial(gather_panels, halves, n) for n, halves in enumerate(((0, 1), (1, 0), (1, 1)))],
        ct, u, strip,
    )
    left, right, norms = finish(
        panel_order,
        pivot_inverses,
        t_all.reshape(2, PW, PW),
        u_all.reshape(2, PW, width),
        ct_all.reshape(2 * PW, ROWS),
        matrix,
        rhs,
    )
    return left, right, norms[0]


def solution(mesh):
    split = Mesh(mesh.devices.reshape(NZ, NC, NY, NX), ("z", "core", "y", "x"))
    rows, cols = ("z", "core"), ("y", "x")
    return jax.shard_map(
        on_device,
        mesh=split,
        in_specs=(P(rows, cols), P(rows, cols), P(), P()),
        out_specs=(P(rows, cols), P(rows, cols), P(cols)),
        check_vma=False,
    )
```

profile of v0, /device:TPU:6, one launch (start us, length us, event | category | flops | bytes accessed | tf_op | source)
XLA Modules:
  0.0 97.7 jit_solution(4717984982288687095)
XLA Ops:
  0.6 0.0 copy-start.6
  0.6 1.4 %multiply_reduce_fusion = s32[]{:T(128)} fusion(s32[2]{0:T(128)} %constant.11.clone, s32[2]{0:T(128)} %order_ref.3), kind=kLoop, calls=%fused_computation.1 | loop fusion | flops 5 | bytes 20 | tf_op jit(solution)/shard_map/reduce_sum | solution.py:546
  2.7 0.0 copy-start
  2.7 1.5 %copy-done = f32[960,480]{1,0:T(8,128)S(1)} copy-done((f32[960,480]{1,0:T(8,128)S(1)}, f32[960,480]{1,0:T(8,128)}, u32[]{:S(2)}) %copy-start) | copy-done | bytes 1843224
  4.2 0.0 copy-start.2
  4.2 1.0 %copy-done.2 = f32[960,128]{1,0:T(8,128)S(1)} copy-done((f32[960,128]{1,0:T(8,128)S(1)}, f32[960,128]{1,0:T(8,128)}, u32[]{:S(2)}) %copy-start.2) | copy-done | bytes 491544
  5.2 0.0 copy-start.5
  5.2 0.7 copy-done.5
  5.9 0.0 copy-start.1
  5.9 0.0 copy-start.3
  5.9 0.0 copy-start.4
  5.9 1.4 %prepare.1 = (f32[2,32,1024]{2,1,0:T(8,128)S(1)}, f32[2,32,640]{2,1,0:T(8,128)S(1)}, f32[2,8,128]{2,1,0:T(8,128)S(1)}) custom-call(s32[2]{0:T(128)S(1)} %copy-done.5, f32[960,480]{1,0:T(8,128)S(1)} %copy-done, f32[960,128]{1,0:T(8,128)S(1)} %copy-done.2), custom_call_target="tpu_custom_call" | custom-call | tf_op jit(solution)/shard_map/prepare/pallas_call | solution.py:528
  7.3 68.9 %conditional.1 = (f32[1024,1024]{1,0:T(8,128)}, f32[2,512,640]{2,1,0:T(8,128)}, f32[2,512,512]{2,1,0:T(8,128)}) conditional(s32[]{:T(128)} %clamp.3, (f32[2,32,1024]{2,1,0:T(8,128)S(1)}, f32[2,32,640]{2,1,0:T(8,128)S(1)}, f32[2,8,128]{2,1,0:T(8,128)S(1)}) %prepare.1, (f32[2,32,1024]{2,1,0:T(8,128)S(1)}, f32[2,32,640]{2,1,0:T(8,128)S(1)}, ...), branch_computations={%region_1.0_spmd, %region_2.0_spmd, %region_3.0_spmd} | conditional | bytes 24 | solution.py:547
  7.3 68.7 %gather_2.1 = (f32[2,16,32,1024]{3,2,1,0:T(8,128)}, f32[2,16,32,640]{3,2,1,0:T(8,128)}, f32[2,16,32,512]{3,2,1,0:T(8,128)}) custom-call(f32[2,32,1024]{2,1,0:T(8,128)S(1)} %get-tuple-element.42.ct_ref, f32[2,32,640]{2,1,0:T(8,128)S(1)} %get-tuple-element.43.u_ref, f32[2,8,128]{2,1,0:T(8,128)S(1)} %get-tuple-element.44.strip_ref), custom_call_target="tpu_custom_call" | custom-call | tf_op jit(solution)/shard_map/cond/branch_2_fun/gather_2/pallas_call | solution.py:327
  76.2 0.0 copy-done.6
  76.2 0.0 copy-done.1
  76.2 0.0 copy-done.3
  76.3 0.0 copy-done.4
  76.3 19.2 %finish.1 = (bf16[960,480]{1,0:T(8,128)(2,1)S(1)}, f32[960,128]{1,0:T(8,128)S(1)}, f32[8,128]{1,0:T(8,128)S(1)}) custom-call(s32[2]{0:T(128)S(1)} %copy-done.6, bf16[2,512,512]{2,1,0:T(8,128)(2,1)S(1)} %copy-done.4, f32[2,512,512]{2,1,0:T(8,128)} %get-tuple-element.57.t_ref, f32[2,512,640]{2,1,0:T(8,128)} %get-tuple-element.58.u_ref, ...), custom_call_target="tpu_custom_call" | custom-call | tf_op jit(solution)/shard_map/finish/pallas_call | solution.py:475
  95.5 0.5 slice_bitcast_fusion
  96.0 0.9 copy.19
  96.9 0.8 copy.20
Async XLA Ops:
  0.6 75.6 %copy-start.6 = (s32[2]{0:T(128)S(1)}, s32[2]{0:T(128)}, u32[]{:S(2)}) copy-start(s32[2]{0:T(128)} %order_ref.3) | copy-start | bytes 28
  2.7 1.5 %copy-start = (f32[960,480]{1,0:T(8,128)S(1)}, f32[960,480]{1,0:T(8,128)}, u32[]{:S(2)}) copy-start(f32[960,480]{1,0:T(8,128)} %a.1) | copy-start | bytes 5529604
  4.2 1.0 %copy-start.2 = (f32[960,128]{1,0:T(8,128)S(1)}, f32[960,128]{1,0:T(8,128)}, u32[]{:S(2)}) copy-start(f32[960,128]{1,0:T(8,128)} %r.1) | copy-start | bytes 1474564
  5.2 0.7 copy-start.5
  5.9 70.3 %copy-start.1 = (f32[960,480]{1,0:T(8,128)S(1)}, f32[960,480]{1,0:T(8,128)}, u32[]{:S(2)}) copy-start(f32[960,480]{1,0:T(8,128)} %a.1) | copy-start | bytes 5529604
  5.9 70.4 %copy-start.3 = (f32[960,128]{1,0:T(8,128)S(1)}, f32[960,128]{1,0:T(8,128)}, u32[]{:S(2)}) copy-start(f32[960,128]{1,0:T(8,128)} %r.1) | copy-start | bytes 1474564
  5.9 70.4 %copy-start.4 = (bf16[2,512,512]{2,1,0:T(8,128)(2,1)S(1)}, bf16[2,512,512]{2,1,0:T(8,128)(2,1)}, u32[]{:S(2)}) copy-start(bf16[2,512,512]{2,1,0:T(8,128)(2,1)} %v_ref.1) | copy-start | bytes 3145732
where the time goes:
time: 98 us; the launch traced here: 97.7 us
  Pallas kernels  89.3 us (91%)
  local copies, waits for them, and re-layouts  5.48 us (6%)
  other arithmetic  1.36 us (1%)
  between operations  1.35 us (1%)
    pallas_call x1, Pallas kernels, gather_panels(): pl.pallas_call(functools.partial(gather_kernel, halves), out_shape=(jax.S...  68.7 us
    pallas_call x1, Pallas kernels, finish(): pl.pallas_call(finish_kernel, out_shape=(jax.ShapeDtypeStruct(matrix.shap...  19.2 us
    unnamed x16, local copies, waits for them, and re-layouts  4.96 us

commit v1 on v0

--- a/solution.py
+++ b/solution.py
@@ -502,7 +502,8 @@
     )(order, inverses, t, u, ct, matrix, rhs)
 
 
-def prepare_kernel(order_ref, a_ref, r_ref, ct_out, u_out, strip_out, wide):
+def prepare_kernel(order_ref, a_ref, r_ref, ct_out, u_out, strip_out, branch_out, wide):
+    branch_out[0] = 2 * (order_ref[0] & 1) + (order_ref[1] & 1) - 1
     row_len, col_len = a_ref.shape
     wide[:row_len, :col_len] = a_ref[...]
     wide[row_len:, :] = jnp.zeros((ROWS - row_len, PW), jnp.float32)
@@ -531,21 +532,20 @@
             jax.ShapeDtypeStruct((2, NB, ROWS), jnp.float32),
             jax.ShapeDtypeStruct((2, NB, PW + rhs.shape[1]), jnp.float32),
             jax.ShapeDtypeStruct((2, 8, 128), jnp.float32),
+            jax.ShapeDtypeStruct((1,), jnp.int32),
         ),
         in_specs=[pl.BlockSpec(memory_space=pltpu.SMEM), vmem, vmem],
-        out_specs=[vmem] * 3,
+        out_specs=[*[vmem] * 3, pl.BlockSpec(memory_space=pltpu.SMEM)],
         scratch_shapes=[pltpu.VMEM((ROWS, PW), jnp.float32)],
-        compiler_params=pltpu.CompilerParams(vmem_limit_bytes=14 * MIB),
         name="prepare",
     )(order, matrix, rhs)
 
 
 def on_device(matrix, rhs, pivot_inverses, panel_order):
     width = PW + rhs.shape[1]
-    ct, u, strip = prepare(panel_order, matrix, rhs)
-    branch = jnp.sum((panel_order & 1) * jnp.array([2, 1], jnp.int32)) - 1
+    ct, u, strip, branch = prepare(panel_order, matrix, rhs)
     ct_all, u_all, t_all = lax.switch(
-        branch, [functools.partial(gather_panels, halves, n) for n, halves in enumerate(((0, 1), (1, 0), (1, 1)))],
+        branch[0], [functools.partial(gather_panels, halves, n) for n, halves in enumerate(((0, 1), (1, 0), (1, 1)))],
         ct, u, strip,
     )
     left, right, norms = finish(

time: 98 us -> 96.1 us (0.981)
  local copies, waits for them, and re-layouts: 5.48 us -> 2.25 us
  Pallas kernels: 89.3 us -> 92 us
  other arithmetic: 1.36 us -> 0 us
    unnamed x16 -> x10, local copies, waits for them, and re-layouts: 4.96 us -> 1.74 us
    pallas_call x1, Pallas kernels: 1.41 us -> 3.38 us  [prepare(): pl.pallas_call(prepare_kernel, out_shape=(jax.ShapeDtypeStruct((2, NB, RO...]
    reduce_sum x1 -> x0, other arithmetic: 1.36 us -> none  [on_device(): branch = jnp.sum((panel_order & 1) * jnp.array([2, 1], jnp.int32)) - 1]
where the time goes in v1:
time: 96.1 us; the launch traced here: 95.9 us
  Pallas kernels  92 us (96%)
  local copies, waits for them, and re-layouts  2.25 us (2%)
  between operations  1.37 us (1%)
    pallas_call x1, Pallas kernels, gather_panels(): pl.pallas_call(functools.partial(gather_kernel, halves), out_shape=(jax.S...  69.6 us
    pallas_call x1, Pallas kernels, finish(): pl.pallas_call(finish_kernel, out_shape=(jax.ShapeDtypeStruct(matrix.shap...  19.1 us
    pallas_call x1, Pallas kernels, prepare(): pl.pallas_call(prepare_kernel, out_shape=(jax.ShapeDtypeStruct((2, NB, RO...  3.38 us

profile of v1, /device:TPU:6, one launch (start us, length us, event | category | flops | bytes accessed | tf_op | source)
XLA Modules:
  0.0 95.9 jit_solution(16343770557459308075)
XLA Ops:
  0.6 0.0 copy-start.3
  0.6 0.0 copy-start.1
  0.7 0.0 copy-start
  0.7 0.0 copy-start.2
  0.7 3.4 %prepare.1 = (f32[2,32,1024]{2,1,0:T(8,128)}, f32[2,32,640]{2,1,0:T(8,128)}, f32[2,8,128]{2,1,0:T(8,128)S(1)}, s32[1]{0:T(128)}) custom-call(s32[2]{0:T(128)} %order_ref.3, f32[960,480]{1,0:T(8,128)} %a.1, f32[960,128]{1,0:T(8,128)} %r.1), custom_call_target="tpu_custom_call" | custom-call | tf_op jit(solution)/shard_map/prepare/pallas_call | solution.py:529
  4.7 69.8 %conditional.1 = (f32[1024,1024]{1,0:T(8,128)}, f32[2,512,640]{2,1,0:T(8,128)}, f32[2,512,512]{2,1,0:T(8,128)}) conditional(s32[]{:T(128)} %bitcast.9, (f32[2,32,1024]{2,1,0:T(8,128)}, f32[2,32,640]{2,1,0:T(8,128)}, f32[2,8,128]{2,1,0:T(8,128)S(1)}) %tuple.29, (f32[2,32,1024]{2,1,0:T(8,128)}, f32[2,32,640]{2,1,0:T(8,128)}, ...), branch_computations={%region_0.0_spmd, %region_1.0_spmd, %region_2.0_spmd} | conditional | bytes 24 | solution.py:547
  4.7 69.6 %gather_2.1 = (f32[2,16,32,1024]{3,2,1,0:T(8,128)}, f32[2,16,32,640]{3,2,1,0:T(8,128)}, f32[2,16,32,512]{3,2,1,0:T(8,128)}) custom-call(f32[2,32,1024]{2,1,0:T(8,128)} %get-tuple-element.42.ct_ref, f32[2,32,640]{2,1,0:T(8,128)} %get-tuple-element.43.u_ref, f32[2,8,128]{2,1,0:T(8,128)S(1)} %get-tuple-element.44.strip_ref), custom_call_target="tpu_custom_call" | custom-call | tf_op jit(solution)/shard_map/cond/branch_2_fun/gather_2/pallas_call | solution.py:327
  74.5 0.0 copy-done.3
  74.5 0.0 copy-done.1
  74.5 0.0 copy-done
  74.5 0.0 copy-done.2
  74.6 19.1 %finish.1 = (bf16[960,480]{1,0:T(8,128)(2,1)S(1)}, f32[960,128]{1,0:T(8,128)S(1)}, f32[8,128]{1,0:T(8,128)S(1)}) custom-call(s32[2]{0:T(128)S(1)} %copy-done.3, bf16[2,512,512]{2,1,0:T(8,128)(2,1)S(1)} %copy-done.2, f32[2,512,512]{2,1,0:T(8,128)} %get-tuple-element.65.t_ref, f32[2,512,640]{2,1,0:T(8,128)} %get-tuple-element.66.u_ref, ...), custom_call_target="tpu_custom_call" | custom-call | tf_op jit(solution)/shard_map/finish/pallas_call | solution.py:475
  93.6 0.5 slice_bitcast_fusion
  94.2 0.9 copy.18
  95.1 0.8 copy.19
Async XLA Ops:
  0.6 73.9 %copy-start.3 = (s32[2]{0:T(128)S(1)}, s32[2]{0:T(128)}, u32[]{:S(2)}) copy-start(s32[2]{0:T(128)} %order_ref.3) | copy-start | bytes 28
  0.6 73.9 %copy-start.1 = (f32[960,128]{1,0:T(8,128)S(1)}, f32[960,128]{1,0:T(8,128)}, u32[]{:S(2)}) copy-start(f32[960,128]{1,0:T(8,128)} %r.1) | copy-start | bytes 1474564
  0.7 73.9 %copy-start = (f32[960,480]{1,0:T(8,128)S(1)}, f32[960,480]{1,0:T(8,128)}, u32[]{:S(2)}) copy-start(f32[960,480]{1,0:T(8,128)} %a.1) | copy-start | bytes 5529604
  0.7 73.9 %copy-start.2 = (bf16[2,512,512]{2,1,0:T(8,128)(2,1)S(1)}, bf16[2,512,512]{2,1,0:T(8,128)(2,1)}, u32[]{:S(2)}) copy-start(bf16[2,512,512]{2,1,0:T(8,128)(2,1)} %v_ref.1) | copy-start | bytes 3145732
